TPU v7x, 32 devices: a whole 2x2x4 slice. The times are simulated.
32 devices in a mesh: grp: 4 (over x, core), row: 4 (over z), col: 2 (over y).
Axes of the slice: x: 2, y: 2, z: 4, core: 2. Of those that a mesh axis runs over, the one named last changes fastest.
Arguments:
- fields: bfloat16 [4, 4, 192, 1536], P('grp', None, 'row', 'col'), may hold values from -12 to 12
- offset: int32 [1], replicated, may hold values from 0 to 191
- level_index: int32 [4], replicated, may hold values from 0 to 3, each once
- nudge_rate: float32 [4], replicated, may hold values from 0.2 to 0.9
- driving: float32 [4, 64, 64], replicated, may hold values from -4 to 4
Outputs:
- nudged: bfloat16 [4, 4, 192, 1536], P('grp', None, 'row', 'col')
Inputs may be any that keep to these rules, and one draw needn't show every extreme that they name: `offset`: the footprint covers a third of the parent rows from there on, wrapping around the periodic domain. `level_index`: each parent level is fed by exactly one child level.
All inputs are finite; a program needn't handle non-finite values.
Results may differ from a plain program's by a relative error of at most 0.0034.
Values may be sent and summed in bfloat16 or wider, within the bound.
A program may use at most 64 MiB of HBM per device.

v0:
```python
import math

import jax
import jax.numpy as jnp
from jax import lax
from jax.sharding import PartitionSpec as P

MAX_WAVE = 32


def from_root(block, axis, source):
    block = jnp.where(lax.axis_index(axis) == source, block, jnp.zeros_like(block))
    return lax.psum(block, axis)


def fourier_table(positions, cell_count, max_order):
    orders = jnp.arange(1, max_order + 1, dtype=jnp.int32)
    period = 3 * cell_count
    phase_index = positions[:, None] * orders[None, :] % period
    angles = phase_index.astype(jnp.float32) * jnp.float32(2.0 * math.pi / period)
    wave_scale = jnp.float32(math.sqrt(2.0 / cell_count))
    constant = jnp.full((positions.shape[0], 1), 1.0 / math.sqrt(cell_count), jnp.float32)
    return jnp.concatenate(
        [constant, wave_scale * jnp.cos(angles), wave_scale * jnp.sin(angles[:, : max_order - 1])],
        axis=1,
    )


def place_rows(carried, block_rows, strip_index):
    height = block_rows.shape[1]
    inside = (strip_index >= 0) & (strip_index < height)
    picked = jnp.take(block_rows, jnp.clip(strip_index, 0, height - 1), axis=1)
    mask_shape = (1, inside.shape[0]) + (1,) * (block_rows.ndim - 2)
    return jnp.where(inside.reshape(mask_shape), picked, carried)


def per_device(fields, offset, level_index, nudge_rate, driving):
    group_id = lax.axis_index("grp")
    row_id = lax.axis_index("row")
    col_id = lax.axis_index("col")
    group_count = lax.axis_size("grp")
    local_slab = fields[0]
    levels, tile_rows, tile_cols = local_slab.shape
    full_rows = lax.axis_size("row") * tile_rows
    full_cols = lax.axis_size("col") * tile_cols
    third_rows = tile_rows // 3
    third_cols = tile_cols // 3
    shift_rows = offset[0]
    is_parent = group_id == group_count - 1
    level_ids = jnp.arange(levels, dtype=jnp.int32)
    inverse = jnp.sum(
        level_ids[:, None] * (level_index[:, None] == level_ids[None, :]).astype(jnp.int32), axis=0
    )
    parent_rows = row_id * tile_rows + jnp.arange(tile_rows, dtype=jnp.int32)
    parent_cols = col_id * tile_cols + jnp.arange(tile_cols, dtype=jnp.int32)
    strip_index = (parent_rows - shift_rows) % full_rows
    covered = strip_index < full_rows // 3
    row_table = fourier_table(3 * parent_rows, full_rows, MAX_WAVE)
    col_table = fourier_table(3 * parent_cols, full_cols, MAX_WAVE)
    row_half = lax.optimization_barrier(row_table.astype(jnp.bfloat16))
    row_rounded = row_half.astype(jnp.float32)
    col_rounded = col_table.astype(jnp.bfloat16)
    block_sums = jnp.sum(
        local_slab.reshape(levels, third_rows, 3, third_cols, 3), axis=(2, 4), dtype=jnp.float32
    )
    averaged = (block_sums / 9.0).astype(jnp.bfloat16)
    by_parent = jnp.take(averaged, inverse, axis=0)
    empty_tile = jnp.zeros((levels, tile_rows, third_cols), jnp.bfloat16)
    placed = place_rows(
        empty_tile, lax.all_gather(by_parent, "row", axis=1, tiled=True), strip_index
    )
    thirds = lax.all_gather(placed[:, :, None, :], "grp", axis=2, tiled=True)
    arrived = thirds[:, :, : group_count - 1, :].reshape(levels, tile_rows, tile_cols)
    fed_tile = jnp.where(covered[None, :, None], arrived, local_slab)
    projected = jnp.einsum("lrc,cm->lrm", fed_tile, col_rounded, preferred_element_type=jnp.float32)
    partial_sums = jnp.einsum(
        "rn,lrm->lnm", row_rounded, projected, precision=lax.Precision.HIGHEST
    )
    summed = lax.psum(partial_sums, ("row", "col"))
    coeffs = from_root(summed, "grp", group_count - 1)
    amplitude = math.sqrt(full_rows * full_cols) / (2 * MAX_WAVE)
    deficit = amplitude * driving - coeffs
    child_rows = (3 * shift_rows + parent_rows - 1) % (3 * full_rows)
    child_cols = (
        (3 * col_id + group_id) * tile_cols + jnp.arange(tile_cols, dtype=jnp.int32) - 1
    ) % (3 * full_cols)
    rows_used = jnp.where(is_parent, row_table, fourier_table(child_rows, full_rows, MAX_WAVE))
    cols_used = jnp.where(is_parent, col_table, fourier_table(child_cols, full_cols, MAX_WAVE))
    level_deficit = jnp.where(is_parent, deficit, jnp.take(deficit, level_index, axis=0))
    level_rate = jnp.where(is_parent, nudge_rate, jnp.take(nudge_rate, level_index, axis=0))
    base_tile = jnp.where(is_parent, fed_tile, local_slab)
    spread_cols = jnp.einsum(
        "lnm,cm->lnc", level_deficit, cols_used, precision=lax.Precision.HIGHEST
    )
    increment = jnp.einsum("rn,lnc->lrc", rows_used, spread_cols, precision=lax.Precision.HIGHEST)
    result = (base_tile.astype(jnp.float32) + level_rate[:, None, None] * increment).astype(
        jnp.bfloat16
    )
    return result[None]


def solution(mesh):
    placed = (P("grp", None, "row", "col"), P(), P(), P(), P())
    return jax.shard_map(
        per_device,
        mesh=mesh,
        in_specs=placed,
        out_specs=P("grp", None, "row", "col"),
        check_vma=False,
    )
```

profile of v0, /device:TPU:0, one launch (start us, length us, event | category | flops | bytes accessed | tf_op | source)
XLA Modules:
  0.0 187.4 jit_solution(7154075441931077724)
XLA Ops:
  6.5 0.0 all-reduce.3.cloned.1.call-start
  6.5 0.7 select_reduce_fusion
  8.0 0.0 copy-start.1
  8.0 0.0 copy-start.3
  8.0 0.0 copy-start
  8.0 0.0 copy-start.2
  8.1 25.9 %reshape.136 = f32[4,16,3,256,3]{4,3,2,1,0:T(8,128)} reshape(bf16[1,4,48,768]{3,2,1,0:T(8,128)(2,1)} %param.5) | data formatting | bytes 884736 | tf_op jit(solution)/shard_map/convert_element_type | solution.py:63
  34.0 11.8 %reduce_sum.21 = f32[4,16,256]{2,1,0:T(8,128)S(1)} reduce(f32[4,16,3,256,3]{4,3,2,1,0:T(8,128)} %reshape.136, f32[]{:T(128)} %constant.140.clone.1), dimensions={2,4}, to_apply=%region_1.2 | reduce | flops 131072 | bytes 655364 | tf_op jit(solution)/shard_map/reduce_sum | solution.py:63
  45.8 0.5 gather_fusion
  46.3 0.1 broadcast_select_fusion.1
  46.4 15.1 %all_gather.6 = bf16[4,64,256]{2,1,0:T(8,128)(2,1)S(1)} all-gather(bf16[4,16,256]{2,1,0:T(8,128)(2,1)S(1)} %broadcast_select_fusion.1), channel_id=1, replica_groups=mesh['grp'=4,'row'=4,'col'=2] {'row'}, dimensions={1}, use_global_device_ids=true | all-gather | bytes 163840 | tf_op jit(solution)/shard_map/all_gather | solution.py:70
  61.5 0.1 copy.20
  61.6 0.7 gather_fusion.1
  62.3 0.1 fusion.24
  62.4 6.5 %all_gather.7 = bf16[4,48,4,256]{3,1,0,2:T(8,128)(2,1)S(1)} all-gather(bf16[4,48,1,256]{3,1,0,2:T(8,128)(2,1)S(1)} %fusion.24), channel_id=1, replica_groups=mesh['grp'=4,'row'=4,'col'=2] {'grp'}, dimensions={2}, use_global_device_ids=true | all-gather | bytes 491520 | tf_op jit(solution)/shard_map/all_gather | solution.py:72
  68.9 0.8 cosine_multiply_fusion.1
  69.7 0.3 fusion.21
  70.1 0.3 cosine_multiply_fusion.2
  70.4 0.1 fusion.40
  70.5 0.1 fusion.55
  70.6 0.0 copy-done.1
  70.6 0.3 fusion.13
  70.9 1.0 convolution_bitcast_fusion
  71.9 0.0 all-reduce.3.cloned.1.call-update
  71.9 0.0 all-reduce.5.cloned.1.call-start
  71.9 0.0 copy-done.3
  72.0 0.3 fusion.20
  72.3 0.1 fusion.39
  72.4 0.0 copy-done
  72.4 0.6 gather_fusion.2
  73.1 70.4 %all-reduce.3.cloned.1.call-done = f32[4,64,64]{1,2,0:T(8,128)} async-done(((f32[4,64,64]{1,2,0:T(8,128)}), f32[4,64,64]{1,2,0:T(8,128)}) %all-reduce.3.cloned.1.call-update) | async-done | bytes 65552 | tf_op jit(solution)/shard_map/psum | solution.py:79
  143.4 0.7 broadcast_select_fusion
  144.1 0.0 all-reduce.5.cloned.1.call-update
  144.1 0.0 copy-done.2
  144.1 0.1 copy.23
  144.2 32.4 %all-reduce.5.cloned.1.call-done = f32[4,64,64]{1,2,0:T(8,128)} async-done(((f32[4,64,64]{1,2,0:T(8,128)}), f32[4,64,64]{1,2,0:T(8,128)}) %all-reduce.5.cloned.1.call-update) | async-done | bytes 65552 | tf_op jit(solution)/shard_map/psum | solution.py:13
  176.6 0.9 multiply_subtract_fusion
  177.6 0.6 gather_fusion.3
  178.1 0.9 fusion.5
  179.1 1.5 fusion.3
  (19 shorter events, 0.2 us)
Async XLA Ops:
  6.5 136.9 %all-reduce.3.cloned.1.call-start = ((), (), s32[]{:S(2)}) async-start(), calls=%async_computation | async-start | bytes 262144 | tf_op jit(solution)/shard_map/psum | solution.py:79
  8.0 62.6 %copy-start.1 = (bf16[1,4,48,768]{3,2,1,0:T(8,128)(2,1)S(1)}, bf16[1,4,48,768]{3,2,1,0:T(8,128)(2,1)}, u32[]{:S(2)}) copy-start(bf16[1,4,48,768]{3,2,1,0:T(8,128)(2,1)} %param.5) | copy-start | bytes 884740
  8.0 63.9 %copy-start.3 = (s32[4]{0:T(128)S(1)}, s32[4]{0:T(128)}, u32[]{:S(2)}) copy-start(s32[4]{0:T(128)} %param.7) | copy-start | bytes 52
  8.0 64.4 %copy-start = (f32[4]{0:T(128)S(1)}, f32[4]{0:T(128)}, u32[]{:S(2)}) copy-start(f32[4]{0:T(128)} %param.8) | copy-start | bytes 52
  8.0 136.1 %copy-start.2 = (f32[4,64,64]{2,1,0:T(8,128)S(1)}, f32[4,64,64]{2,1,0:T(8,128)}, u32[]{:S(2)}) copy-start(f32[4,64,64]{2,1,0:T(8,128)} %param.9) | copy-start | bytes 196612
  71.9 104.8 %all-reduce.5.cloned.1.call-start = ((), (), s32[]{:S(2)}) async-start(), calls=%async_computation.1 | async-start | bytes 262144 | tf_op jit(solution)/shard_map/psum | solution.py:13
Sparse Core Ops, SparseCore 0:
  72.0 71.3 all-reduce.2
  145.7 30.8 all-reduce.4
where the time goes:
time: 188 us; the launch traced here: 187 us
  waiting for transfers between devices  103 us (55%)
  local copies, waits for them, and re-layouts  28.6 us (15%)
  blocking collectives  21.5 us (11%)
  other arithmetic  16.5 us (9%)
  between operations  14.3 us (8%)
  matrix products  3.65 us (2%)
    psum x1, waiting for transfers between devices, per_device(): summed = lax.psum(partial_sums, ('row', 'col'))  70.4 us
    psum x1, waiting for transfers between devices, from_root(): return lax.psum(block, axis)  32.4 us
    convert_element_type x1, local copies, waits for them, and re-layouts, per_device(): jnp.sum(local_slab.reshape(levels, third_rows, 3, third_cols, 3), axis=(2...  25.9 us
    all_gather x1, blocking collectives, per_device(): lax.all_gather(by_parent, 'row', axis=1, tiled=True)  15.1 us
    reduce_sum x1, other arithmetic, per_device(): jnp.sum(local_slab.reshape(levels, third_rows, 3, third_cols, 3), axis=(2...  11.8 us
    all_gather x1, blocking collectives, per_device(): thirds = lax.all_gather(placed[:, :, None, :], 'grp', axis=2, tiled=True)  6.46 us
  transfers between devices with their start and end apart: 2, of which 2 were waited for; matrix products, arithmetic and copies ran while one was open for 1% of the time, Pallas kernels for 0%

commit v1 on v0

v1 whole, which is shorter than its diff:
```python
import functools
import math

import jax
import jax.numpy as jnp
from jax import lax
from jax.experimental import pallas as pl
from jax.experimental.pallas import tpu as pltpu
from jax.sharding import PartitionSpec as P

MESH = pl.DeviceIdType.MESH
F32, BF16 = jnp.float32, jnp.bfloat16


def count(shape, axis):
    return lax.broadcasted_iota(jnp.int32, shape, axis).astype(F32)


def split(index, size):
    whole = jnp.floor((index + 0.5) * (1.0 / size))
    return whole, index - size * whole


def basis(order, position, cells, top):
    period = 3 * cells
    is_sine = order > top
    wave = 4.0 * jnp.where(is_sine, order - top, order)
    phase = wave * position - jnp.where(is_sine, float(period), 0.0)
    turn = 4.0 * period
    phase = phase - turn * jnp.floor(phase * (1.0 / turn) + 0.5)
    t = (period - jnp.abs(phase)) * (math.pi / (2.0 * period))
    t2 = t * t
    poly = 1.0 / math.factorial(13)
    for degree in (11, 9, 7, 5, 3, 1):
        sign = -1.0 if degree % 4 == 3 else 1.0
        poly = poly * t2 + sign / math.factorial(degree)
    scale = jnp.where(order == 0, 1.0 / math.sqrt(cells), math.sqrt(2.0 / cells))
    return scale * (poly * t)


def halves(value):
    high = value.astype(BF16)
    return high, (value - high.astype(F32)).astype(BF16)


def dot(a, b):
    return jnp.dot(a, b, preferred_element_type=F32)


def kernel(
    sizes, offset_ref, level_ref, rate_ref, fields_ref, driving_ref, out_ref,
    tile, average, base, sent, got, passed, crossed, whole, placed_in, row_mix, col_mix, drive,
    load_sem, s1, r1, s2, r2, s3, r3, sf, rf,
):
    groups, rows, cols = sizes
    group, row, col = lax.axis_index("grp"), lax.axis_index("row"), lax.axis_index("col")
    levels, tile_rows, tile_cols = tile.shape
    size = driving_ref.shape[1]
    top = size // 2
    full_rows, full_cols = rows * tile_rows, cols * tile_cols
    third_rows, third_cols = tile_rows // 3, tile_cols // 3
    flat = levels * tile_rows
    strip = levels * third_rows
    plane = groups * cols
    pairs = levels // 2
    chunk = pairs * size // plane
    parent = groups - 1
    is_parent = group == parent
    mine = group * cols + col

    def plane_peer(step):
        other = lax.rem(mine + step, plane)
        return other, (other // cols, row, lax.rem(other, cols))

    load = pltpu.make_async_copy(fields_ref.at[0], tile, load_sem)
    load.start()

    barrier = pltpu.get_barrier_semaphore()
    for step in range(1, plane):
        pl.semaphore_signal(barrier, 1, device_id=plane_peer(step)[1], device_id_type=MESH)
    for turn in range(1, rows):
        for other in range(groups):
            pl.semaphore_signal(
                barrier, 1, device_id=(other, lax.rem(row + turn, rows), col), device_id_type=MESH
            )

    shift = offset_ref[0].astype(F32)
    row_f, col_f, group_f = row.astype(F32), col.astype(F32), group.astype(F32)

    def lookup(index, values):
        out = jnp.where(index == 0, values[0], values[1])
        for n in range(2, levels):
            out = jnp.where(index == n, values[n], out)
        return out

    targets = [level_ref[n].astype(F32) for n in range(levels)]
    rates = [rate_ref[n] for n in range(levels)]

    load.wait()

    def store_partial(mix, projected):
        high, low = halves(projected)
        coeffs = dot(mix, high) + dot(mix, low)
        lane = count((size, 2 * size), 1)
        for pair in range(pairs):
            first = coeffs[2 * pair * size : (2 * pair + 1) * size]
            second = coeffs[(2 * pair + 1) * size : (2 * pair + 2) * size]
            both = jnp.where(lane < size, first, second)
            for n in range(size // chunk):
                sent[pair * (size // chunk) + n] = both[n * chunk : (n + 1) * chunk]

    @pl.when(jnp.logical_not(is_parent))
    def _():
        d = count((tile_cols, third_cols), 0) - 3.0 * count((tile_cols, third_cols), 1)
        pick = jnp.where((d >= 0) & (d < 3), 1.0, 0.0).astype(BF16)
        summed = dot(tile[...].reshape(flat, tile_cols), pick)
        level, i = split(count((1, flat), 1), tile_rows)
        land = lookup(level, targets) * third_rows + split(i, 3)[0]
        mix = jnp.where(count((strip, flat), 0) == land, 1.0, 0.0).astype(BF16)
        high = summed.astype(BF16)
        rest = summed - high.astype(F32)
        middle, low = halves(rest)
        total = dot(mix, high) + dot(mix, middle) + dot(mix, low)
        block = (total / 9.0).astype(BF16)
        average[...] = block
        x = (3.0 * col_f + group_f) * third_cols + count((third_cols, 2 * size), 0)
        order = split(count((1, 2 * size), 1), size)[1]
        projected = dot(block, basis(order, 3.0 * x, full_cols, top).astype(BF16))
        level_to, order_to = split(count((levels * size, 1), 0), size)
        level_from, q = split(count((1, strip), 1), third_rows)
        r = row_f * third_rows + q + shift
        table = basis(order_to, 3.0 * r, full_rows, top)
        store_partial(jnp.where(level_to == level_from, table, 0.0).astype(BF16), projected)

    @pl.when(is_parent)
    def _():
        x = col_f * tile_cols + count((tile_cols, 2 * size), 0)
        order = split(count((1, 2 * size), 1), size)[1]
        table = basis(order, 3.0 * x, full_cols, top).astype(BF16)
        projected = dot(tile[...].reshape(flat, tile_cols), table)
        level_to, order_to = split(count((levels * size, 1), 0), size)
        level_from, i = split(count((1, flat), 1), tile_rows)
        r = row_f * tile_rows + i
        s = r - shift
        s = jnp.where(s < 0, s + full_rows, s)
        table = basis(order_to, 3.0 * r, full_rows, top)
        keep = (level_to == level_from) & (s >= full_rows // 3)
        store_partial(jnp.where(keep, table, 0.0).astype(BF16), projected)

    pl.semaphore_wait(barrier, plane - 1 + (rows - 1) * groups)

    scatter = []
    for step in range(1, plane):
        other, device = plane_peer(step)
        copy = pltpu.make_async_remote_copy(
            src_ref=sent.at[other], dst_ref=got.at[step - 1], send_sem=s1.at[step - 1],
            recv_sem=r1.at[step - 1], device_id=device, device_id_type=MESH,
        )
        copy.start()
        scatter.append(copy)

    def feed(g, turn, source, target):
        return pltpu.make_async_remote_copy(
            src_ref=average,
            dst_ref=placed_in.at[source, :, pl.ds(pl.multiple_of(g * third_cols, 128), third_cols)],
            send_sem=sf.at[turn], recv_sem=rf.at[g * rows + turn],
            device_id=(parent, target, col), device_id_type=MESH,
        )

    @pl.when(jnp.logical_not(is_parent))
    def _():
        for turn in range(rows):
            feed(group, turn, row, lax.rem(row + turn, rows)).start()

    level, i = split(count((flat, 1), 0), tile_rows)
    at = jnp.where(is_parent, level, lookup(level, targets))
    pair_at, half_at = split(at, 2)
    pair, order = split(count((1, pairs * size), 1), size)
    i = i + row_f * tile_rows
    z = jnp.where(is_parent, 3.0 * i, 3.0 * shift + i - 1.0)
    table = basis(order, z, full_rows, top) * lookup(at, rates)
    row_high, row_low = halves(jnp.where(pair == pair_at, table, 0.0))
    row_mix[0] = row_high
    row_mix[1] = row_low

    j = count((1, tile_cols), 1)
    z = jnp.where(
        is_parent, 3.0 * (col_f * tile_cols + j), (3.0 * col_f + group_f) * tile_cols + j - 1.0
    )
    col_high, col_low = halves(basis(count((size, 1), 0), z, full_cols, top))
    col_mix[0] = col_high
    col_mix[1] = col_high
    col_mix[2] = col_low
    col_mix[3] = col_low
    amplitude = math.sqrt(full_rows * full_cols) / size
    for pair_n in range(pairs):
        drive[pair_n] = amplitude * jnp.concatenate(
            [driving_ref[2 * pair_n], driving_ref[2 * pair_n + 1]], axis=1
        )

    total = sent[mine]
    for step in range(1, plane):
        scatter[step - 1].wait_recv()
        total = total + got[step - 1]
    passed[...] = total
    along = []
    for turn in range(1, rows):
        copy = pltpu.make_async_remote_copy(
            src_ref=passed, dst_ref=crossed.at[turn - 1], send_sem=s2.at[turn - 1],
            recv_sem=r2.at[turn - 1], device_id=(group, lax.rem(row + turn, rows), col),
            device_id_type=MESH,
        )
        copy.start()
        along.append(copy)
    for turn in range(1, rows):
        along[turn - 1].wait_recv()
        total = total + crossed[turn - 1]
    whole[mine] = total
    gather = []
    for step in range(1, plane):
        other, device = plane_peer(step)
        copy = pltpu.make_async_remote_copy(
            src_ref=whole.at[mine], dst_ref=whole.at[mine], send_sem=s3.at[step - 1],
            recv_sem=r3.at[step - 1], device_id=device, device_id_type=MESH,
        )
        copy.start()
        gather.append(copy)

    @pl.when(is_parent)
    def _():
        for g in range(groups - 1):
            for turn in range(rows):
                feed(g, turn, lax.rem(row + rows - turn, rows), row).wait_recv()
        level_to, i = split(count((flat, 1), 0), tile_rows)
        s = row_f * tile_rows + i - shift
        s = jnp.where(s < 0, s + full_rows, s)
        source, rest = split(count((1, rows * strip), 1), strip)
        level_from, q = split(rest, third_rows)
        hit = (level_to == level_from) & (s == source * third_rows + q)
        pick = jnp.where(hit, 1.0, 0.0).astype(BF16)
        arrived = dot(pick, placed_in[...].reshape(rows * strip, tile_cols)).astype(BF16)
        own = tile[...].reshape(flat, tile_cols)
        fed = jnp.where(s < full_rows // 3, arrived.astype(F32), own.astype(F32)).astype(BF16)
        base[...] = fed

    @pl.when(jnp.logical_not(is_parent))
    def _():
        base[...] = tile[...].reshape(flat, tile_cols)

    for step in range(1, plane):
        came = lax.rem(mine + plane - step, plane)
        pltpu.make_async_remote_copy(
            src_ref=whole.at[mine], dst_ref=whole.at[came], send_sem=s3.at[step - 1],
            recv_sem=r3.at[step - 1], device_id=plane_peer(step)[1], device_id_type=MESH,
        ).wait_recv()

    coeffs = jnp.concatenate([whole[n] for n in range(plane)], axis=0)
    deficit = drive[...].reshape(pairs * size, 2 * size) - coeffs
    high, low = halves(deficit)
    spread = dot(row_mix[0], high) + dot(row_mix[0], low) + dot(row_mix[1], high)
    lane_half = split(count((1, 2 * size), 1), size)[0]
    spread = jnp.where(lane_half == half_at, spread, 0.0)
    spread = spread + pltpu.roll(spread, size, 1)
    rounded = spread.astype(BF16).astype(F32)
    parts = jnp.where(lane_half == 0, rounded, spread - rounded).astype(BF16)
    mixed = jnp.concatenate([parts, parts], axis=1)
    increment = dot(mixed, col_mix[...].reshape(4 * size, tile_cols))
    result = (base[...].astype(F32) + increment).astype(BF16)
    out_ref[...] = result.reshape(1, levels, tile_rows, tile_cols)

    for copy in scatter + along + gather:
        copy.wait_send()

    @pl.when(jnp.logical_not(is_parent))
    def _():
        for turn in range(rows):
            feed(group, turn, row, lax.rem(row + turn, rows)).wait_send()


def solution(mesh):
    groups, rows, cols = (mesh.shape[name] for name in ("grp", "row", "col"))
    plane = groups * cols

    def per_device(fields, offset, level_index, nudge_rate, driving):
        _, levels, tile_rows, tile_cols = fields.shape
        size = driving.shape[1]
        strip = levels * tile_rows // 3
        flat = levels * tile_rows
        pairs = levels // 2
        chunk = pairs * size // plane
        dma = lambda n: pltpu.SemaphoreType.DMA((n,))
        vmem = pl.BlockSpec(memory_space=pltpu.VMEM)
        smem = pl.BlockSpec(memory_space=pltpu.SMEM)
        return pl.pallas_call(
            functools.partial(kernel, (groups, rows, cols)),
            out_shape=jax.ShapeDtypeStruct(fields.shape, fields.dtype),
            in_specs=[smem, smem, smem, pl.BlockSpec(memory_space=pl.ANY), vmem],
            out_specs=vmem,
            scratch_shapes=[
                pltpu.VMEM((levels, tile_rows, tile_cols), BF16),
                pltpu.VMEM((strip, tile_cols // 3), BF16),
                pltpu.VMEM((flat, tile_cols), BF16),
                pltpu.VMEM((plane, chunk, 2 * size), F32),
                pltpu.VMEM((plane - 1, chunk, 2 * size), F32),
                pltpu.VMEM((chunk, 2 * size), F32),
                pltpu.VMEM((rows - 1, chunk, 2 * size), F32),
                pltpu.VMEM((plane, chunk, 2 * size), F32),
                pltpu.VMEM((rows, strip, tile_cols), BF16),
                pltpu.VMEM((2, flat, pairs * size), BF16),
                pltpu.VMEM((4, size, tile_cols), BF16),
                pltpu.VMEM((pairs, size, 2 * size), F32),
                pltpu.SemaphoreType.DMA,
                dma(plane - 1), dma(plane - 1), dma(rows - 1), dma(rows - 1),
                dma(plane - 1), dma(plane - 1), dma(rows), dma((groups - 1) * rows),
            ],
            compiler_params=pltpu.CompilerParams(collective_id=0, has_side_effects=True),
        )(offset, level_index, nudge_rate, fields, driving)

    placed = (P("grp", None, "row", "col"), P(), P(), P(), P())
    return jax.shard_map(
        per_device,
        mesh=mesh,
        in_specs=placed,
        out_specs=P("grp", None, "row", "col"),
        check_vma=False,
    )
```

time: 188 us -> 22.1 us (0.12)
  waiting for transfers between devices: 103 us -> 0 us
  local copies, waits for them, and re-layouts: 28.6 us -> 1.69 us
  blocking collectives: 21.5 us -> 0 us
  Pallas kernels: 0 us -> 19.5 us
  other arithmetic: 16.5 us -> 0 us
  between operations: 14.3 us -> 0.66 us
  matrix products: 3.65 us -> 0 us
    psum x2 -> x0, waiting for transfers between devices: 103 us -> none  [the longest x1 70.4 us: per_device(): summed = lax.psum(partial_sums, ('row', 'col'))]
    convert_element_type x1 -> x0, local copies, waits for them, and re-layouts: 25.9 us -> none  [per_device(): jnp.sum(local_slab.reshape(levels, third_rows, 3, third_cols, 3), axis=(2...]
    all_gather x2 -> x0, blocking collectives: 21.5 us -> none  [the longest x1 15.1 us: per_device(): lax.all_gather(by_parent, 'row', axis=1, tiled=True)]
    pallas_call x0 -> x1, Pallas kernels: none -> 19.5 us  [per_device(): pl.pallas_call(functools.partial(kernel, (groups, rows, cols)), out_shape...]
    reduce_sum x2 -> x0, other arithmetic: 12.5 us -> none  [the longest x1 11.8 us: per_device(): jnp.sum(local_slab.reshape(levels, third_rows, 3, third_cols, 3), axis=(2...]
    dot_general x4 -> x0, matrix products: 3.65 us -> none  [the longest x1 1.48 us: per_device(): jnp.einsum('rn,lnc->lrc', rows_used, spread_cols, precision=lax.Precision...]
    gather x4 -> x0, local copies, waits for them, and re-layouts: 2.4 us -> none  [the longest x1 0.66 us: place_rows(): picked = jnp.take(block_rows, jnp.clip(strip_index, 0, height - 1), axis=1)]
    mul x6 -> x0, other arithmetic: 1.96 us -> none  [the longest x2 1.1 us: fourier_table(): wave_scale * jnp.cos(angles)]
  transfers between devices with their start and end apart: 2 -> 0, of which waited for: 2 -> 0; matrix products, arithmetic and copies ran while one was open for 1% -> 0% of each run, Pallas kernels for 0% -> 0%
where the time goes in v1:
time: 22.1 us; the launch traced here: 21.9 us
  Pallas kernels  19.5 us (88%)
  local copies, waits for them, and re-layouts  1.69 us (8%)
  between operations  0.66 us (3%)
    pallas_call x1, Pallas kernels, per_device(): pl.pallas_call(functools.partial(kernel, (groups, rows, cols)), out_shape...  19.5 us
    unnamed x1, local copies, waits for them, and re-layouts  1.69 us

profile of v1, /device:TPU:0, one launch (start us, length us, event | category | flops | bytes accessed | tf_op | source)
XLA Modules:
  0.0 21.9 jit_solution(15644443773424449950)
XLA Ops:
  0.7 19.5 %shard_map.55 = bf16[1,4,48,768]{3,2,1,0:T(8,128)(2,1)} custom-call(s32[1]{0:T(128)S(6)} %copy.7.offset_ref, s32[4]{0:T(128)} %level_ref.1, f32[4]{0:T(128)} %rate_ref.1, bf16[1,4,48,768]{3,2,1,0:T(8,128)(2,1)} %fields_ref.1, f32[4,64,64]{2,1,0:T(8,128)} %driving_ref.1), custom_call_target="tpu_custom_call" | custom-call | tf_op jit(solution)/shard_map/pallas_call | solution.py:294
  20.2 1.7 %copy.8 = bf16[1,4,48,768]{3,2,1,0:T(8,128)(2,1)} copy(bf16[1,4,48,768]{3,2,1,0:T(8,128)(2,1)} %shard_map.55) | data formatting | bytes 589824

commit v2 on v1

--- a/solution.py
+++ b/solution.py
@@ -48,9 +48,9 @@
 
 
 def kernel(
-    sizes, offset_ref, level_ref, rate_ref, fields_ref, driving_ref, out_ref,
-    tile, average, base, sent, got, passed, crossed, whole, placed_in, row_mix, col_mix, drive,
-    load_sem, s1, r1, s2, r2, s3, r3, sf, rf,
+    sizes, offset_hbm, level_hbm, rate_hbm, fields_ref, driving_hbm, out_ref,
+    offset_ref, level_ref, rate_ref, driving_ref, tile, average, base, sent, got, passed, crossed, whole, placed_in, row_mix, col_mix, drive,
+    load_sem, few_sem, drive_sem, s1, r1, s2, r2, s3, r3, sf, rf,
 ):
     groups, rows, cols = sizes
     group, row, col = lax.axis_index("grp"), lax.axis_index("row"), lax.axis_index("col")
@@ -74,6 +74,15 @@
 
     load = pltpu.make_async_copy(fields_ref.at[0], tile, load_sem)
     load.start()
+    few = [
+        pltpu.make_async_copy(offset_hbm, offset_ref, few_sem.at[0]),
+        pltpu.make_async_copy(level_hbm, level_ref, few_sem.at[1]),
+        pltpu.make_async_copy(rate_hbm, rate_ref, few_sem.at[2]),
+    ]
+    for copy in few:
+        copy.start()
+    load_drive = pltpu.make_async_copy(driving_hbm, driving_ref, drive_sem)
+    load_drive.start()
 
     barrier = pltpu.get_barrier_semaphore()
     for step in range(1, plane):
@@ -84,6 +93,8 @@
                 barrier, 1, device_id=(other, lax.rem(row + turn, rows), col), device_id_type=MESH
             )
 
+    for copy in few:
+        copy.wait()
     shift = offset_ref[0].astype(F32)
     row_f, col_f, group_f = row.astype(F32), col.astype(F32), group.astype(F32)
 
@@ -95,8 +106,6 @@
 
     targets = [level_ref[n].astype(F32) for n in range(levels)]
     rates = [rate_ref[n] for n in range(levels)]
-
-    load.wait()
 
     def store_partial(mix, projected):
         high, low = halves(projected)
@@ -113,31 +122,31 @@
     def _():
         d = count((tile_cols, third_cols), 0) - 3.0 * count((tile_cols, third_cols), 1)
         pick = jnp.where((d >= 0) & (d < 3), 1.0, 0.0).astype(BF16)
-        summed = dot(tile[...].reshape(flat, tile_cols), pick)
         level, i = split(count((1, flat), 1), tile_rows)
         land = lookup(level, targets) * third_rows + split(i, 3)[0]
         mix = jnp.where(count((strip, flat), 0) == land, 1.0, 0.0).astype(BF16)
+        x = (3.0 * col_f + group_f) * third_cols + count((third_cols, 2 * size), 0)
+        order = split(count((1, 2 * size), 1), size)[1]
+        col_table = basis(order, 3.0 * x, full_cols, top).astype(BF16)
+        level_to, order_to = split(count((levels * size, 1), 0), size)
+        level_from, q = split(count((1, strip), 1), third_rows)
+        table = basis(order_to, 3.0 * (row_f * third_rows + q + shift), full_rows, top)
+        row_table = jnp.where(level_to == level_from, table, 0.0).astype(BF16)
+        load.wait()
+        summed = dot(tile[...].reshape(flat, tile_cols), pick)
         high = summed.astype(BF16)
         rest = summed - high.astype(F32)
         middle, low = halves(rest)
         total = dot(mix, high) + dot(mix, middle) + dot(mix, low)
         block = (total / 9.0).astype(BF16)
         average[...] = block
-        x = (3.0 * col_f + group_f) * third_cols + count((third_cols, 2 * size), 0)
-        order = split(count((1, 2 * size), 1), size)[1]
-        projected = dot(block, basis(order, 3.0 * x, full_cols, top).astype(BF16))
-        level_to, order_to = split(count((levels * size, 1), 0), size)
-        level_from, q = split(count((1, strip), 1), third_rows)
-        r = row_f * third_rows + q + shift
-        table = basis(order_to, 3.0 * r, full_rows, top)
-        store_partial(jnp.where(level_to == level_from, table, 0.0).astype(BF16), projected)
+        store_partial(row_table, dot(block, col_table))
 
     @pl.when(is_parent)
     def _():
         x = col_f * tile_cols + count((tile_cols, 2 * size), 0)
         order = split(count((1, 2 * size), 1), size)[1]
-        table = basis(order, 3.0 * x, full_cols, top).astype(BF16)
-        projected = dot(tile[...].reshape(flat, tile_cols), table)
+        col_table = basis(order, 3.0 * x, full_cols, top).astype(BF16)
         level_to, order_to = split(count((levels * size, 1), 0), size)
         level_from, i = split(count((1, flat), 1), tile_rows)
         r = row_f * tile_rows + i
@@ -145,7 +154,9 @@
         s = jnp.where(s < 0, s + full_rows, s)
         table = basis(order_to, 3.0 * r, full_rows, top)
         keep = (level_to == level_from) & (s >= full_rows // 3)
-        store_partial(jnp.where(keep, table, 0.0).astype(BF16), projected)
+        row_table = jnp.where(keep, table, 0.0).astype(BF16)
+        load.wait()
+        store_partial(row_table, dot(tile[...].reshape(flat, tile_cols), col_table))
 
     pl.semaphore_wait(barrier, plane - 1 + (rows - 1) * groups)
 
@@ -166,11 +177,6 @@
             send_sem=sf.at[turn], recv_sem=rf.at[g * rows + turn],
             device_id=(parent, target, col), device_id_type=MESH,
         )
-
-    @pl.when(jnp.logical_not(is_parent))
-    def _():
-        for turn in range(rows):
-            feed(group, turn, row, lax.rem(row + turn, rows)).start()
 
     level, i = split(count((flat, 1), 0), tile_rows)
     at = jnp.where(is_parent, level, lookup(level, targets))
@@ -193,6 +199,7 @@
     col_mix[2] = col_low
     col_mix[3] = col_low
     amplitude = math.sqrt(full_rows * full_cols) / size
+    load_drive.wait()
     for pair_n in range(pairs):
         drive[pair_n] = amplitude * jnp.concatenate(
             [driving_ref[2 * pair_n], driving_ref[2 * pair_n + 1]], axis=1
@@ -212,6 +219,11 @@
         )
         copy.start()
         along.append(copy)
+    @pl.when(jnp.logical_not(is_parent))
+    def _():
+        for turn in range(rows):
+            feed(group, turn, row, lax.rem(row + turn, rows)).start()
+
     for turn in range(1, rows):
         along[turn - 1].wait_recv()
         total = total + crossed[turn - 1]
@@ -289,14 +301,17 @@
         pairs = levels // 2
         chunk = pairs * size // plane
         dma = lambda n: pltpu.SemaphoreType.DMA((n,))
-        vmem = pl.BlockSpec(memory_space=pltpu.VMEM)
-        smem = pl.BlockSpec(memory_space=pltpu.SMEM)
+        here = pl.BlockSpec(memory_space=pl.ANY)
         return pl.pallas_call(
             functools.partial(kernel, (groups, rows, cols)),
             out_shape=jax.ShapeDtypeStruct(fields.shape, fields.dtype),
-            in_specs=[smem, smem, smem, pl.BlockSpec(memory_space=pl.ANY), vmem],
-            out_specs=vmem,
+            in_specs=[here] + [pl.BlockSpec(memory_space=pltpu.HBM)] * 4,
+            out_specs=pl.BlockSpec(memory_space=pltpu.VMEM),
             scratch_shapes=[
+                pltpu.SMEM(offset.shape, offset.dtype),
+                pltpu.SMEM(level_index.shape, level_index.dtype),
+                pltpu.SMEM(nudge_rate.shape, nudge_rate.dtype),
+                pltpu.VMEM(driving.shape, driving.dtype),
                 pltpu.VMEM((levels, tile_rows, tile_cols), BF16),
                 pltpu.VMEM((strip, tile_cols // 3), BF16),
                 pltpu.VMEM((flat, tile_cols), BF16),
@@ -309,12 +324,17 @@
                 pltpu.VMEM((2, flat, pairs * size), BF16),
                 pltpu.VMEM((4, size, tile_cols), BF16),
                 pltpu.VMEM((pairs, size, 2 * size), F32),
-                pltpu.SemaphoreType.DMA,
+                pltpu.SemaphoreType.DMA, dma(3), pltpu.SemaphoreType.DMA,
                 dma(plane - 1), dma(plane - 1), dma(rows - 1), dma(rows - 1),
                 dma(plane - 1), dma(plane - 1), dma(rows), dma((groups - 1) * rows),
             ],
-            compiler_params=pltpu.CompilerParams(collective_id=0, has_side_effects=True),
-        )(offset, level_index, nudge_rate, fields, driving)
+            compiler_params=pltpu.CompilerParams(
+                collective_id=0, has_side_effects=True, vmem_limit_bytes=36 * 2**20
+            ),
+        )(
+            offset,
+            *(pltpu.with_memory_space_constraint(v, pltpu.HBM) for v in (level_index, nudge_rate, fields, driving)),
+        )
 
     placed = (P("grp", None, "row", "col"), P(), P(), P(), P())
     return jax.shard_map(

time: 22.1 us -> 18.1 us (0.82)
  Pallas kernels: 19.5 us -> 16.6 us
  local copies, waits for them, and re-layouts: 1.69 us -> 0.72 us
    pallas_call x1, Pallas kernels: 19.5 us -> 16.6 us  [per_device(): pl.pallas_call(functools.partial(kernel, (groups, rows, cols)), out_shape...]
    unnamed x1, local copies, waits for them, and re-layouts: 1.69 us -> 0.72 us
where the time goes in v2:
time: 18.1 us; the launch traced here: 18 us
  Pallas kernels  16.6 us (92%)
  local copies, waits for them, and re-layouts  0.72 us (4%)
  between operations  0.66 us (4%)
    pallas_call x1, Pallas kernels, per_device(): pl.pallas_call(functools.partial(kernel, (groups, rows, cols)), out_shape...  16.6 us
    unnamed x1, local copies, waits for them, and re-layouts  0.72 us

profile of v2, /device:TPU:0, one launch (start us, length us, event | category | flops | bytes accessed | tf_op | source)
XLA Modules:
  0.0 18.0 jit_solution(7025654468551138719)
XLA Ops:
  0.7 16.6 %shard_map.55 = bf16[1,4,48,768]{3,2,1,0:T(8,128)(2,1)S(1)} custom-call(s32[1]{0:T(128)S(6)} %copy.7.offset_hbm, s32[4]{0:T(128)} %level_hbm.1, f32[4]{0:T(128)} %rate_hbm.1, bf16[1,4,48,768]{3,2,1,0:T(8,128)(2,1)} %fields_ref.1, f32[4,64,64]{2,1,0:T(8,128)} %driving_hbm.1), custom_call_target="tpu_custom_call" | custom-call | tf_op jit(solution)/shard_map/pallas_call | solution.py:305
  17.2 0.7 %copy.8 = bf16[1,4,48,768]{3,2,1,0:T(8,128)(2,1)} copy(bf16[1,4,48,768]{3,2,1,0:T(8,128)(2,1)S(1)} %shard_map.55) | data formatting | bytes 589824
